TPU v7x, 32 devices: a whole 2x2x4 slice. The times are simulated.
32 devices in a mesh: dp: 4 (over x, core), fsdp: 4 (over z), mp: 2 (over y).
Axes of the slice: x: 2, y: 2, z: 4, core: 2. Of those that a mesh axis runs over, the one named last changes fastest.
Arguments:
- tokens_in: bfloat16 [4096, 3072], P(('dp', 'fsdp', 'mp')), may hold values from -40 to 40
- segment_ids: int32 [4096], P(('dp', 'fsdp', 'mp')), may hold values from 0 to 31, never falling along the last dimension, each value on 1 to 512 neighbouring positions
- target_ids: int32 [4096], P(('dp', 'fsdp', 'mp')), may hold values from 0 to 8191
- old_weights: bfloat16 [4, 3072, 2048], P(None, ('dp', 'fsdp', 'mp'))
- old_first: float32 [4, 3072, 2048], P(None, ('dp', 'fsdp', 'mp')), may hold values from -6 to 6
- old_second: float32 [4, 3072, 2048], P(None, ('dp', 'fsdp', 'mp')), may hold values from 0.01 to 4
- old_block: int32 [32], P(('dp', 'fsdp', 'mp')), may hold values from 0 to 31, each once
- new_residue: int32 [4], P('dp'), may hold values from 0 to 3, each once
- norm_gain: float32 [3072], replicated, may hold values from 0.5 to 1.5
- head_weight: bfloat16 [3072, 8192], P(None, ('fsdp', 'mp'))
Outputs:
- new_weights: bfloat16 [4, 3072, 2048], P(None, 'dp', ('fsdp', 'mp'))
- new_first: float32 [4, 3072, 2048], P(None, 'dp', ('fsdp', 'mp'))
- new_second: float32 [4, 3072, 2048], P(None, 'dp', ('fsdp', 'mp'))
- loss: float32 [4096], P(('dp', 'fsdp', 'mp'))
Inputs may be any that keep to these rules, and one draw needn't show every extreme that they name: `old_block`: a permutation of the old layout's row blocks. `new_residue`: a permutation; index i of dp holds the rows whose number modulo 4 is new_residue[i], in rising order. `segment_ids`: never falling along the tokens.
All inputs are finite; a program needn't handle non-finite values.
Results may differ from a plain program's by a relative error of at most 0.0075.
Values may be sent and summed in bfloat16 or wider, within the bound.
A program may use at most 192 MiB of HBM per device.

v0:
```python
import math

import jax
import jax.numpy as jnp
from jax import lax
from jax.sharding import PartitionSpec as P

HD = 128


def combined_all(part, axis, combine):
    gathered = jax.tree.map(lambda a: lax.all_gather(a, axis), part)

    def take(source):
        return jax.tree.map(lambda a: lax.dynamic_index_in_dim(a, source, 0, False), gathered)

    return lax.fori_loop(
        1, lax.axis_size(axis), lambda source, state: combine(state, take(source)), take(0)
    )


def inverse_of(table):
    total_count = table.shape[0]
    places = jnp.arange(total_count, dtype=jnp.int32)
    return jnp.sum(jnp.where(table[None, :] == places[:, None], places[None, :], 0), axis=1)


def pack_rows(stored, residues, fm_count):
    matrices, row_count, columns = stored.shape
    dp_count = residues.shape[0]
    split_rows = stored.reshape(
        matrices, row_count // dp_count, dp_count, fm_count, columns // fm_count
    )
    chosen = jnp.take(split_rows, residues, axis=2)
    return chosen.transpose(2, 3, 0, 1, 4).reshape(
        dp_count * fm_count, matrices, row_count // dp_count, columns // fm_count
    )


def unpack_rows(received, holder):
    ordered = jnp.take(received, holder, axis=0)
    devices, matrices, pair_rows, group_cols = ordered.shape
    return ordered.transpose(1, 0, 2, 3).reshape(matrices, devices * pair_rows, group_cols)


def norm_rows(hidden, norm_gain):
    scale = lax.rsqrt(jnp.mean(hidden * hidden, axis=1, keepdims=True) + 1e-05)
    return (hidden * scale * norm_gain).astype(jnp.bfloat16)


def combine_parts(earlier, later):
    joint_max = jnp.maximum(earlier[0], later[0])
    joint_total = earlier[1] * jnp.exp(earlier[0] - joint_max) + later[1] * jnp.exp(
        later[0] - joint_max
    )
    return (joint_max, joint_total, earlier[2] + later[2])


def body(
    tokens_in,
    segment_ids,
    target_ids,
    old_weights,
    old_first,
    old_second,
    old_block,
    new_residue,
    norm_gain,
    head_weight,
):
    dp_count = lax.axis_size("dp")
    fm_count = lax.axis_size(("fsdp", "mp"))
    matrices, old_rows, columns = old_weights.shape
    group_cols = columns // fm_count
    table_all = lax.all_gather(old_block, ("dp", "fsdp", "mp"), axis=0, tiled=True)
    residues = lax.all_gather(new_residue, "dp", axis=0, tiled=True)
    holder = inverse_of(table_all)
    first_sent = pack_rows(old_first, residues, fm_count)
    second_sent = pack_rows(old_second, residues, fm_count)
    first_got, second_got = (
        lax.all_to_all(first_sent, ("dp", "fsdp", "mp"), split_axis=0, concat_axis=0, tiled=True),
        lax.all_to_all(second_sent, ("dp", "fsdp", "mp"), split_axis=0, concat_axis=0, tiled=True),
    )
    new_first = unpack_rows(first_got, holder)
    new_second = unpack_rows(second_got, holder)
    whole_tokens = lax.all_gather(tokens_in, ("fsdp", "mp"), axis=0, tiled=True)
    segments, targets = (
        lax.all_gather(segment_ids, ("fsdp", "mp"), axis=0, tiled=True),
        lax.all_gather(target_ids, ("fsdp", "mp"), axis=0, tiled=True),
    )
    seq_len, model_width = whole_tokens.shape
    new_rows = model_width // dp_count
    weights_sent = pack_rows(old_weights, residues, fm_count)
    weights_got = lax.all_to_all(
        weights_sent, ("dp", "fsdp", "mp"), split_axis=0, concat_axis=0, tiled=True
    )
    new_weights = unpack_rows(weights_got, holder)
    piece = lax.all_gather(new_weights[:3], "dp", axis=1, tiled=True)
    positions = jnp.arange(piece.shape[1], dtype=jnp.int32)
    feature_ids = jnp.take(residues, positions // new_rows) + dp_count * (positions % new_rows)
    picked_cols = jnp.take(whole_tokens, feature_ids, axis=1)
    projected = jnp.einsum("sr,mrc->msc", picked_cols, piece, preferred_element_type=jnp.float32)
    heads = group_cols // HD
    queries = projected[0].astype(jnp.bfloat16).reshape(seq_len, heads, HD)
    keys_all = projected[1].astype(jnp.bfloat16).reshape(seq_len, heads, HD)
    values_all = projected[2].astype(jnp.bfloat16).reshape(seq_len, heads, HD)
    positions_all = jnp.arange(seq_len, dtype=jnp.int32)
    allowed = (positions_all[:, None] >= positions_all[None, :]) & (
        segments[:, None] == segments[None, :]
    )
    scores = jnp.einsum("shd,thd->hst", queries, keys_all, preferred_element_type=jnp.float32) * (
        1.0 / math.sqrt(HD)
    )
    scores = jnp.where(allowed[None], scores, -1e30)
    row_max = jnp.max(scores, axis=2, keepdims=True)
    expo = jnp.where(allowed[None], jnp.exp(scores - row_max), 0.0)
    soft = (expo / jnp.sum(expo, axis=2, keepdims=True)).astype(jnp.bfloat16)
    attended = jnp.einsum("hst,thd->shd", soft, values_all, preferred_element_type=jnp.float32)
    attended = attended.astype(jnp.bfloat16).reshape(seq_len, group_cols)
    shuffled = jnp.einsum(
        "sc,rc->sr",
        attended,
        lax.all_gather(new_weights[3], "dp", axis=0, tiled=True),
        preferred_element_type=jnp.float32,
    )
    inverse_res = inverse_of(residues)
    partial_value = jnp.take(shuffled.reshape(seq_len, dp_count, new_rows), inverse_res, axis=1)
    partial_value = partial_value.transpose(0, 2, 1).reshape(seq_len, model_width)
    own_sum = lax.psum_scatter(
        partial_value.astype(jnp.bfloat16), ("fsdp", "mp"), scatter_dimension=0, tiled=True
    ).astype(jnp.float32)
    own_normed = norm_rows(tokens_in.astype(jnp.float32) + own_sum, norm_gain)
    normed = lax.all_gather(own_normed, ("fsdp", "mp"), axis=0, tiled=True)
    logits = jnp.dot(normed, head_weight, preferred_element_type=jnp.float32)
    vocab_dev = logits.shape[1]
    offset = lax.axis_index(("fsdp", "mp")) * vocab_dev
    row_top = jnp.max(logits, axis=1)
    row_total = jnp.sum(jnp.exp(logits - row_top[:, None]), axis=1)
    vocab_ids = jnp.arange(vocab_dev, dtype=jnp.int32) + offset
    picked = jnp.sum(jnp.where(vocab_ids[None, :] == targets[:, None], logits, 0.0), axis=1)
    joint_max, joint_total, joint_picked = combined_all(
        (row_top, row_total, picked), ("fsdp", "mp"), combine_parts
    )
    token_loss = joint_max + jnp.log(joint_total) - joint_picked
    own_count = tokens_in.shape[0]
    own_start = lax.axis_index(("fsdp", "mp")) * own_count
    loss = lax.dynamic_slice_in_dim(token_loss, own_start, own_count)
    return (new_weights, new_first, new_second, loss)


def solution(mesh):
    placed = (
        P(("dp", "fsdp", "mp"), None),
        P(("dp", "fsdp", "mp")),
        P(("dp", "fsdp", "mp")),
        P(None, ("dp", "fsdp", "mp"), None),
        P(None, ("dp", "fsdp", "mp"), None),
        P(None, ("dp", "fsdp", "mp"), None),
        P(("dp", "fsdp", "mp")),
        P("dp"),
        P(),
        P(None, ("fsdp", "mp")),
    )
    return jax.shard_map(
        body,
        mesh=mesh,
        in_specs=placed,
        out_specs=(
            P(None, "dp", ("fsdp", "mp")),
            P(None, "dp", ("fsdp", "mp")),
            P(None, "dp", ("fsdp", "mp")),
            P(("dp", "fsdp", "mp")),
        ),
        check_vma=False,
    )
```

profile of v0, /device:TPU:0, one launch (start us, length us, event | category | flops | bytes accessed | tf_op | source)
XLA Modules:
  0.0 690.0 jit_solution(11615841543775525765)
XLA Ops:
  12.3 6.4 all-reduce.1
  21.7 5.2 all-to-all-start
  27.8 80.9 %all-reduce = s32[32]{0:T(128)S(1)} all-reduce(s32[32]{0:T(128)S(1)} %dynamic-update-slice), channel_id=1, replica_groups=mesh['dp'=4,'fsdp'=4,'mp'=2] {'dp','fsdp','mp'}, use_global_device_ids=true, to_apply=%add | all-reduce | flops 32 | bytes 256
  111.6 25.4 %all-gather.3 = s32[8,1,128]{2,1,0:T(1,128)S(1)} all-gather(s32[1,1,128]{2,1,0:T(1,128)S(1)} %bitcast.122), channel_id=1, replica_groups=mesh['dp'=4,'fsdp'=4,'mp'=2] {'fsdp','mp'}, dimensions={0}, use_global_device_ids=true | all-gather | bytes 4608 | tf_op jit(solution)/shard_map/all_gather | solution.py:88
  141.9 19.5 %gather_fusion.2 = bf16[3072,1024]{1,0:T(8,128)(2,1)} fusion(bf16[1024,3072]{0,1:T(8,128)(2,1)} %all-gather.12.cloned.1.call-done, s32[3072]{0:T(1024)S(1)} %broadcast_clamp_fusion), kind=kCustom, calls=%fused_computation.6 | custom fusion | bytes 12595200 | tf_op jit(solution)/shard_map/jit(_take)/gather | solution.py:101
  161.4 17.3 %all-gather.10.cloned.1.call-done = bf16[3,3072,256]{1,2,0:T(8,128)(2,1)} async-done(((bf16[3,768,256]{1,2,0:T(8,128)(2,1)}), bf16[3,3072,256]{1,2,0:T(8,128)(2,1)}) %all-gather.10.cloned.1.call-update) | async-done | bytes 4718608 | tf_op jit(solution)/shard_map/all_gather | solution.py:98
  178.6 9.3 %fusion.16 = bf16[3,1024,256]{1,2,0:T(8,128)(2,1)S(1)} fusion(bf16[3,3072,256]{1,2,0:T(8,128)(2,1)} %all-gather.10.cloned.1.call-done, bf16[3072,1024]{1,0:T(8,128)(2,1)} %gather_fusion.2, pred[3072]{0:T(1024)(128)(4,1)S(1)} %compare_and_fusion), kind=kOutput, calls=%fused_computation.42 | convolution fusion | flops 4835770368 | bytes 12585984 | tf_op jit(solution)/shard_map/sr,mrc->msc/dot_general | solution.py:102
  189.1 8.7 %fusion.40 = (f32[2,1024]{1,0:T(2,128)S(1)}, f32[2,1024,1024]{1,2,0:T(8,128)}) fusion(pred[1024,1024]{0,1:T(8,128)(4,1)S(1)} %fusion.9, bf16[1024,2,128]{0,2,1:T(8,128)(2,1)} %bitcast.114, bf16[1024,2,128]{0,2,1:T(8,128)(2,1)} %bitcast.113), kind=kOutput, calls=%fused_computation.101 | convolution fusion | flops 547357696 | bytes 10493952 | tf_op jit(solution)/shard_map/sub | solution.py:116
  197.7 4.1 fusion.19
  201.9 5.9 fusion.42
  207.8 6.4 gather_fusion.3
  214.2 7.2 %fusion.2 = bf16[1024,768,4]{1,0,2:T(8,128)(2,1)} fusion(bf16[4,1024,768]{2,1,0:T(8,128)(2,1)} %gather_fusion.3, pred[4]{0:T(512)(128)(4,1)S(1)} %compare_and_fusion.1), kind=kLoop, calls=%fused_computation.18 | loop fusion | flops 3145728 | bytes 12582916 | tf_op jit(solution)/shard_map/convert_element_type | solution.py:130
  221.4 11.5 %copy.74 = bf16[1024,768,4]{0,2,1:T(4,128)(2,1)} copy(bf16[1024,768,4]{1,0,2:T(8,128)(2,1)} %fusion.2) | data formatting | bytes 12582912 | tf_op jit(solution)/shard_map/convert_element_type | solution.py:130
  232.8 9.7 %convert_element_type.51 = bf16[1024,3072]{0,1:T(8,128)(2,1)} reshape(bf16[1024,768,4]{0,2,1:T(4,128)(2,1)} %copy.74) | data formatting | bytes 12582912 | tf_op jit(solution)/shard_map/convert_element_type | solution.py:130
  242.6 8.6 %copy.80 = bf16[1024,3072]{1,0:T(8,128)(2,1)} copy(bf16[1024,3072]{0,1:T(8,128)(2,1)} %convert_element_type.51) | data formatting | bytes 12582912
  251.2 5.0 copy.84
  256.2 4.3 gather_fusion.6
  260.5 5.0 copy.83
  265.5 4.4 gather_fusion.4
  269.9 5.2 select_bitcast_fusion.1
  277.7 5.0 all-to-all-start.2
  282.8 135.5 %reduce-scatter.4.cloned.1.call-done = bf16[128,3072]{1,0:T(8,128)(2,1)} async-done(((bf16[1024,3072]{1,0:T(8,128)(2,1)}), bf16[128,3072]{1,0:T(8,128)(2,1)}) %reduce-scatter.4.cloned.1.call-update) | async-done | bytes 786448
  421.6 4.5 copy.62
  426.1 4.0 all-to-all-start.1
  430.1 91.4 %all-gather.4 = s32[8,1,128]{2,1,0:T(1,128)S(1)} all-gather(s32[1,1,128]{2,1,0:T(1,128)S(1)} %bitcast.123), channel_id=1, replica_groups=mesh['dp'=4,'fsdp'=4,'mp'=2] {'fsdp','mp'}, dimensions={0}, use_global_device_ids=true | all-gather | bytes 4608 | tf_op jit(solution)/shard_map/all_gather | solution.py:89
  525.4 29.2 %all-to-all-done.1 = f32[32,4,24,256]{3,2,1,0:T(8,128)} async-done(((f32[32,4,24,256]{3,2,1,0:T(8,128)}), f32[32,4,24,256]{3,2,1,0:T(8,128)}, u32[]{:S(2)}, u32[]{:S(2)}) %all-to-all-start.1) | async-done | bytes 3145760 | tf_op jit(solution)/shard_map/all_to_all | solution.py:81
  554.6 4.3 gather_fusion.5
  565.6 12.6 %all-gather.16.cloned.1.call-done = bf16[1024,3072]{0,1:T(8,128)(2,1)} async-done(((bf16[128,3072]{0,1:T(8,128)(2,1)}), bf16[1024,3072]{0,1:T(8,128)(2,1)}) %all-gather.16.cloned.1.call-update) | async-done | bytes 6291472 | tf_op jit(solution)/shard_map/all_gather | solution.py:133
  578.2 10.7 %fusion.41 = (f32[1024]{0:T(1024)S(1)}, f32[1024,1024]{0,1:T(8,128)S(1)}) fusion(bf16[1024,3072]{0,1:T(8,128)(2,1)} %all-gather.16.cloned.1.call-done, bf16[3072,1024]{1,0:T(8,128)(2,1)} %param.25), kind=kOutput, calls=%fused_computation.102 | convolution fusion | flops 6443498496 | bytes 16781312 | tf_op jit(solution)/shard_map/dot_general | solution.py:134
  590.3 30.6 %all-gather.1 = f32[8192]{0:T(1024)S(1)} all-gather(f32[1024]{0:T(1024)S(1)} %get-tuple-element.188), channel_id=3, replica_groups=mesh['dp'=4,'fsdp'=4,'mp'=2] {'fsdp','mp'}, dimensions={0}, use_global_device_ids=true | all-gather | bytes 36864 | tf_op jit(solution)/shard_map/all_gather | solution.py:12
  620.9 30.6 %all-gather.2 = f32[8192]{0:T(1024)S(1)} all-gather(f32[1024]{0:T(1024)S(1)} %get-tuple-element.187), channel_id=4, replica_groups=mesh['dp'=4,'fsdp'=4,'mp'=2] {'fsdp','mp'}, dimensions={0}, use_global_device_ids=true | all-gather | bytes 36864 | tf_op jit(solution)/shard_map/all_gather | solution.py:12
  651.6 30.6 %all-gather = f32[8192]{0:T(1024)S(1)} all-gather(f32[1024]{0:T(1024)S(1)} %get-tuple-element.220), channel_id=2, replica_groups=mesh['dp'=4,'fsdp'=4,'mp'=2] {'fsdp','mp'}, dimensions={0}, use_global_device_ids=true | all-gather | bytes 36864 | tf_op jit(solution)/shard_map/all_gather | solution.py:12
  (108 shorter events, 35.9 us)
Async XLA Ops:
  7.2 11.5 %copy-start.1 = (bf16[4,96,2048]{2,1,0:T(8,128)(2,1)S(1)}, bf16[4,96,2048]{2,1,0:T(8,128)(2,1)}, u32[]{:S(2)}) copy-start(bf16[4,96,2048]{2,1,0:T(8,128)(2,1)} %param.19) | copy-start | bytes 4718596
  7.2 134.7 %all-gather.12.cloned.1.call-start = ((), (), s32[]{:S(2)}) async-start(), calls=%async_computation.5 | async-start | bytes 7077888 | tf_op jit(solution)/shard_map/all_gather | solution.py:86
  21.7 87.1 %all-to-all-start = ((bf16[32,4,24,256]{3,2,1,0:T(8,128)(2,1)}), bf16[32,4,24,256]{3,2,1,0:T(8,128)(2,1)S(1)}, u32[]{:S(2)}, u32[]{:S(2)}) async-start(bf16[32,4,24,256]{3,2,1,0:T(8,128)(2,1)} %bitcast.5), calls=%async_computation | async-start | bytes 3145728 | tf_op jit(solution)/shard_map/all_to_all | solution.py:94
  27.0 151.7 %all-gather.10.cloned.1.call-start = ((), (), s32[]{:S(2)}) async-start(), calls=%async_computation.4 | async-start | bytes 5898240 | tf_op jit(solution)/shard_map/all_gather | solution.py:98
  109.8 1.7 copy-start.3
  111.5 90.4 %all-gather.14.cloned.1.call-start = ((), (), s32[]{:S(2)}) async-start(), calls=%async_computation.6 | async-start | bytes 1966080 | tf_op jit(solution)/shard_map/all_gather | solution.py:123
  141.8 276.5 %reduce-scatter.4.cloned.1.call-start = ((), (), s32[]{:S(2)}) async-start(), calls=%async_computation.8 | async-start | bytes 7077888
  277.7 142.0 %copy-start = (bf16[128,3072]{0,1:T(8,128)(2,1)S(1)}, bf16[128,3072]{0,1:T(8,128)(2,1)}, u32[]{:S(2)}) copy-start(bf16[128,3072]{0,1:T(8,128)(2,1)} %copy.66) | copy-start | bytes 2359300
  277.7 148.4 %all-to-all-start.2 = ((f32[32,4,24,256]{3,2,1,0:T(8,128)}), f32[32,4,24,256]{3,2,1,0:T(8,128)}, u32[]{:S(2)}, u32[]{:S(2)}) async-start(f32[32,4,24,256]{3,2,1,0:T(8,128)} %bitcast.98), calls=%async_computation.2 | async-start | bytes 6291456 | tf_op jit(solution)/shard_map/all_to_all | solution.py:82
  282.7 137.5 %copy-start.2 = (f32[3072]{0:T(1024)S(1)}, f32[3072]{0:T(1024)}, u32[]{:S(2)}) copy-start(f32[3072]{0:T(1024)} %param.24) | copy-start | bytes 36868
  282.7 295.5 %all-gather.16.cloned.1.call-start = ((), (), s32[]{:S(2)}) async-start(), calls=%async_computation.7 | async-start | bytes 7077888 | tf_op jit(solution)/shard_map/all_gather | solution.py:133
  426.1 4.0 copy-start.4
  426.1 128.5 %all-to-all-start.1 = ((f32[32,4,24,256]{3,2,1,0:T(8,128)}), f32[32,4,24,256]{3,2,1,0:T(8,128)}, u32[]{:S(2)}, u32[]{:S(2)}) async-start(f32[32,4,24,256]{3,2,1,0:T(8,128)} %bitcast.97), calls=%async_computation.1 | async-start | bytes 6291456 | tf_op jit(solution)/shard_map/all_to_all | solution.py:81
Sparse Core Ops, SparseCore 0:
  10.0 130.7 all-gather.11
  143.0 35.5 all-gather.9
  180.8 19.6 all-gather.13
  251.3 166.8 reduce-scatter.3
  421.7 156.4 all-gather.15
where the time goes:
time: 692 us; the launch traced here: 690 us
  blocking collectives  296 us (43%)
  waiting for transfers between devices  195 us (28%)
  local copies, waits for them, and re-layouts  108 us (16%)
  matrix products  38.7 us (6%)
  other arithmetic  22.4 us (3%)
  between operations  15.4 us (2%)
  starting transfers between devices  14.4 us (2%)
    unnamed x6, waiting for transfers between devices  136 us
    all_gather x3, blocking collectives, combined_all(): gathered = jax.tree.map(lambda a: lax.all_gather(a, axis), part)  91.8 us
    all_gather x1, blocking collectives, body(): lax.all_gather(target_ids, ('fsdp', 'mp'), axis=0, tiled=True)  91.4 us
    unnamed x2, blocking collectives  87.3 us
    all_to_all x1, waiting for transfers between devices, body(): lax.all_to_all(first_sent, ('dp', 'fsdp', 'mp'), split_axis=0, concat_axi...  29.2 us
    all_gather x1, blocking collectives, body(): lax.all_gather(segment_ids, ('fsdp', 'mp'), axis=0, tiled=True)  25.4 us
    unnamed x21, local copies, waits for them, and re-layouts  25.1 us
    convert_element_type x2, local copies, waits for them, and re-layouts, body(): partial_value.astype(jnp.bfloat16)  21.2 us
  transfers between devices with their start and end apart: 8, of which 4 were waited for; matrix products, arithmetic and copies ran while one was open for 15% of the time, Pallas kernels for 0%

commit v1 on v0

v1 whole, which is shorter than its diff:
```python
import math

import jax
import jax.numpy as jnp
from jax import lax
from jax.sharding import PartitionSpec as P

HD = 128


def inverse_of(table):
    total_count = table.shape[0]
    places = jnp.arange(total_count, dtype=jnp.int32)
    return jnp.sum(jnp.where(table[None, :] == places[:, None], places[None, :], 0), axis=1)


def pack_rows(stored, residues, fm_count):
    matrices, row_count, columns = stored.shape
    dp_count = residues.shape[0]
    split_rows = stored.reshape(
        matrices, row_count // dp_count, dp_count, fm_count, columns // fm_count
    )
    chosen = jnp.take(split_rows, residues, axis=2, mode="clip")
    return chosen.transpose(2, 3, 0, 1, 4).reshape(
        dp_count * fm_count, matrices, row_count // dp_count, columns // fm_count
    )


def unpack_rows(received, holder):
    ordered = jnp.take(received, holder, axis=0, mode="clip")
    devices, matrices, pair_rows, group_cols = ordered.shape
    return ordered.transpose(1, 0, 2, 3).reshape(matrices, devices * pair_rows, group_cols)


def norm_rows(hidden, norm_gain):
    scale = lax.rsqrt(jnp.mean(hidden * hidden, axis=1, keepdims=True) + 1e-05)
    return (hidden * scale * norm_gain).astype(jnp.bfloat16)


FLAGS = dict(tail="a2a", first="before_rs", second="free", tokens="first")


def share_tables(segment_ids, target_ids, old_block, new_residue):
    axes = ("dp", "fsdp", "mp")
    own = jnp.concatenate([segment_ids, target_ids, old_block, new_residue])
    rows = jnp.broadcast_to(own[None, None], (lax.axis_size(axes), 1, own.shape[0]))
    rows = lax.all_to_all(rows, axes, split_axis=0, concat_axis=0, tiled=True)[:, 0]
    count = segment_ids.shape[0]
    fm_count = lax.axis_size(("fsdp", "mp"))
    here = lax.dynamic_slice_in_dim(rows, lax.axis_index("dp") * fm_count, fm_count)
    segments = here[:, :count].reshape(-1)
    targets = here[:, count : 2 * count].reshape(-1)
    return segments, targets, rows[:, 2 * count], rows[::fm_count, 2 * count + 1]


def joint_loss(row_top, row_total, picked):
    axes = ("fsdp", "mp")
    fm_count = lax.axis_size(axes)
    parts = jnp.stack([row_top, row_total, picked])
    own_count = parts.shape[1] // fm_count
    if FLAGS["tail"] == "a2a":
        parts = parts.reshape(3, fm_count, own_count).transpose(1, 0, 2)
        parts = lax.all_to_all(parts, axes, split_axis=0, concat_axis=0, tiled=True)
    else:
        place = lax.axis_index(axes)
        rows = jnp.zeros((fm_count,) + parts.shape, jnp.float32)
        rows = lax.psum(lax.dynamic_update_slice(rows, parts[None], (place, 0, 0)), axes)
        parts = lax.dynamic_slice_in_dim(rows, place * own_count, own_count, axis=2)
    tops, totals, targets = parts[:, 0], parts[:, 1], parts[:, 2]
    joint_max = jnp.max(tops, axis=0)
    joint_total = jnp.sum(totals * jnp.exp(tops - joint_max[None]), axis=0)
    return joint_max + jnp.log(joint_total) - jnp.sum(targets, axis=0)


def body(
    tokens_in,
    segment_ids,
    target_ids,
    old_weights,
    old_first,
    old_second,
    old_block,
    new_residue,
    norm_gain,
    head_weight,
):
    dp_count = lax.axis_size("dp")
    fm_count = lax.axis_size(("fsdp", "mp"))
    everyone = ("dp", "fsdp", "mp")
    columns = old_weights.shape[2]
    group_cols = columns // fm_count
    model_width = tokens_in.shape[1]
    new_rows = model_width // dp_count
    segments, targets, table_all, residues = share_tables(
        segment_ids, target_ids, old_block, new_residue
    )
    holder = inverse_of(table_all)
    inverse_res = inverse_of(residues)
    feature_ids = (
        residues[:, None] + dp_count * jnp.arange(new_rows, dtype=jnp.int32)[None]
    ).reshape(-1)
    logical_ids = (
        jnp.arange(new_rows, dtype=jnp.int32)[:, None] + new_rows * inverse_res[None]
    ).reshape(-1)
    own_picked = jnp.take(tokens_in, feature_ids, axis=1, mode="clip")
    picked_cols = lax.all_gather(own_picked, ("fsdp", "mp"), axis=0, tiled=True)
    seq_len = picked_cols.shape[0]
    weights_sent = pack_rows(old_weights, residues, fm_count)
    weights_got = lax.all_to_all(
        weights_sent, everyone, split_axis=0, concat_axis=0, tiled=True
    )
    first_sent = pack_rows(old_first, residues, fm_count)
    second_sent = pack_rows(old_second, residues, fm_count)
    if FLAGS["first"] != "free":
        weights_got, first_sent, second_sent = lax.optimization_barrier(
            (weights_got, first_sent, second_sent)
        )
    new_weights = unpack_rows(weights_got, holder)
    projections = new_weights[:3]
    if FLAGS.get("tokens") == "first":
        picked_cols, projections, first_sent = lax.optimization_barrier(
            (picked_cols, projections, first_sent)
        )
    first_got = lax.all_to_all(first_sent, everyone, split_axis=0, concat_axis=0, tiled=True)
    piece = lax.all_gather(projections, "dp", axis=1, tiled=True)
    projected = jnp.einsum("sr,mrc->msc", picked_cols, piece, preferred_element_type=jnp.float32)
    heads = group_cols // HD
    queries = projected[0].astype(jnp.bfloat16).reshape(seq_len, heads, HD)
    keys_all = projected[1].astype(jnp.bfloat16).reshape(seq_len, heads, HD)
    values_all = projected[2].astype(jnp.bfloat16).reshape(seq_len, heads, HD)
    positions_all = jnp.arange(seq_len, dtype=jnp.int32)
    allowed = (positions_all[:, None] >= positions_all[None, :]) & (
        segments[:, None] == segments[None, :]
    )
    scores = jnp.einsum("shd,thd->hst", queries, keys_all, preferred_element_type=jnp.float32) * (
        1.0 / math.sqrt(HD)
    )
    scores = jnp.where(allowed[None], scores, -1e30)
    row_max = jnp.max(scores, axis=2, keepdims=True)
    expo = jnp.where(allowed[None], jnp.exp(scores - row_max), 0.0)
    soft = (expo / jnp.sum(expo, axis=2, keepdims=True)).astype(jnp.bfloat16)
    attended = jnp.einsum("hst,thd->shd", soft, values_all, preferred_element_type=jnp.float32)
    attended = attended.astype(jnp.bfloat16).reshape(seq_len, group_cols)
    shuffled = jnp.einsum(
        "sc,rc->sr",
        attended,
        lax.all_gather(new_weights[3], "dp", axis=0, tiled=True),
        preferred_element_type=jnp.float32,
    )
    partial_value = shuffled.astype(jnp.bfloat16)
    if FLAGS["first"] == "rs_first":
        partial_value, second_sent = lax.optimization_barrier((partial_value, second_sent))
    if FLAGS["first"] == "before_rs":
        partial_value, first_got, second_sent = lax.optimization_barrier(
            (partial_value, first_got, second_sent)
        )
    second_got = lax.all_to_all(second_sent, everyone, split_axis=0, concat_axis=0, tiled=True)
    own_sum = lax.psum_scatter(
        partial_value, ("fsdp", "mp"), scatter_dimension=0, tiled=True
    )
    own_sum = jnp.take(own_sum, logical_ids, axis=1, mode="clip").astype(jnp.float32)
    own_normed = norm_rows(tokens_in.astype(jnp.float32) + own_sum, norm_gain)
    if FLAGS["second"] == "before_ag":
        own_normed, second_got = lax.optimization_barrier((own_normed, second_got))
    new_first = unpack_rows(first_got, holder)
    new_second = unpack_rows(second_got, holder)
    normed = lax.all_gather(own_normed, ("fsdp", "mp"), axis=0, tiled=True)
    logits = jnp.dot(normed, head_weight, preferred_element_type=jnp.float32)
    vocab_dev = logits.shape[1]
    offset = lax.axis_index(("fsdp", "mp")) * vocab_dev
    row_top = jnp.max(logits, axis=1)
    row_total = jnp.sum(jnp.exp(logits - row_top[:, None]), axis=1)
    vocab_ids = jnp.arange(vocab_dev, dtype=jnp.int32) + offset
    picked = jnp.sum(jnp.where(vocab_ids[None, :] == targets[:, None], logits, 0.0), axis=1)
    loss = joint_loss(row_top, row_total, picked)
    return (new_weights, new_first, new_second, loss)


def solution(mesh):
    placed = (
        P(("dp", "fsdp", "mp"), None),
        P(("dp", "fsdp", "mp")),
        P(("dp", "fsdp", "mp")),
        P(None, ("dp", "fsdp", "mp"), None),
        P(None, ("dp", "fsdp", "mp"), None),
        P(None, ("dp", "fsdp", "mp"), None),
        P(("dp", "fsdp", "mp")),
        P("dp"),
        P(),
        P(None, ("fsdp", "mp")),
    )
    return jax.shard_map(
        body,
        mesh=mesh,
        in_specs=placed,
        out_specs=(
            P(None, "dp", ("fsdp", "mp")),
            P(None, "dp", ("fsdp", "mp")),
            P(None, "dp", ("fsdp", "mp")),
            P(("dp", "fsdp", "mp")),
        ),
        check_vma=False,
    )
```

time: 692 us -> 590 us (0.85)
  blocking collectives: 296 us -> 0 us
  waiting for transfers between devices: 195 us -> 419 us
  local copies, waits for them, and re-layouts: 108 us -> 85.3 us
  other arithmetic: 22.4 us -> 8.52 us
  starting transfers between devices: 14.4 us -> 22.9 us
    all_gather x5 -> x0, blocking collectives: 209 us -> none  [the longest x3 91.8 us: combined_all(): gathered = jax.tree.map(lambda a: lax.all_gather(a, axis), part)]
    all_gather x1, waiting for transfers between devices: 12.6 us -> 149 us  [body(): normed = lax.all_gather(own_normed, ('fsdp', 'mp'), axis=0, tiled=True)]
    unnamed x6 -> x5, waiting for transfers between devices: 136 us -> 0.08 us
    reduce_scatter x0 -> x1, waiting for transfers between devices: none -> 119 us  [body(): lax.psum_scatter(partial_value, ('fsdp', 'mp'), scatter_dimension=0, tile...]
    all_gather x2, waiting for transfers between devices: 17.3 us -> 107 us  [the longest x1 56.2 us: body(): piece = lax.all_gather(projections, 'dp', axis=1, tiled=True)]
    unnamed x2 -> x0, blocking collectives: 87.3 us -> none
    convert_element_type x2 -> x0, local copies, waits for them, and re-layouts: 21.2 us -> none  [body(): partial_value.astype(jnp.bfloat16)]
    unnamed x21 -> x14, local copies, waits for them, and re-layouts: 25.1 us -> 12.8 us
  transfers between devices with their start and end apart: 8 -> 10, of which waited for: 4 -> 7; matrix products, arithmetic and copies ran while one was open for 15% -> 17% of each run, Pallas kernels for 0% -> 0%
where the time goes in v1:
time: 590 us; the launch traced here: 589 us
  waiting for transfers between devices  419 us (71%)
  local copies, waits for them, and re-layouts  85.3 us (14%)
  matrix products  38.1 us (6%)
  starting transfers between devices  22.9 us (4%)
  between operations  15.3 us (3%)
  other arithmetic  8.52 us (1%)
    all_gather x1, waiting for transfers between devices, body(): normed = lax.all_gather(own_normed, ('fsdp', 'mp'), axis=0, tiled=True)  149 us
    reduce_scatter x1, waiting for transfers between devices, body(): lax.psum_scatter(partial_value, ('fsdp', 'mp'), scatter_dimension=0, tile...  119 us
    all_gather x1, waiting for transfers between devices, body(): piece = lax.all_gather(projections, 'dp', axis=1, tiled=True)  56.2 us
    all_gather x1, waiting for transfers between devices, body(): picked_cols = lax.all_gather(own_picked, ('fsdp', 'mp'), axis=0, tiled=True)  50.7 us
    all_to_all x1, waiting for transfers between devices, body(): lax.all_to_all(weights_sent, everyone, split_axis=0, concat_axis=0, tiled...  34 us
    unnamed x14, local copies, waits for them, and re-layouts  12.8 us
    transpose x3, local copies, waits for them, and re-layouts, pack_rows(): chosen.transpose(2, 3, 0, 1, 4)  12.3 us
  transfers between devices with their start and end apart: 10, of which 7 were waited for; matrix products, arithmetic and copies ran while one was open for 17% of the time, Pallas kernels for 0%

profile of v1, /device:TPU:0, one launch (start us, length us, event | category | flops | bytes accessed | tf_op | source)
XLA Modules:
  0.0 589.0 jit_solution(5896758327097351042)
XLA Ops:
  9.9 7.3 %all-to-all-start = ((s32[32,1,258]{2,1,0:T(1,128)}), s32[32,1,258]{2,1,0:T(1,128)S(1)}, u32[]{:S(2)}, u32[]{:S(2)}) async-start(s32[32,1,258]{2,1,0:T(1,128)} %broadcast_in_dim.85), calls=%async_computation | async-start | bytes 98304 | tf_op jit(solution)/shard_map/all_to_all | solution.py:47
  18.8 5.7 all-to-all-done
  24.7 11.4 %gather_fusion.4 = bf16[3072,128]{1,0:T(8,128)(2,1)} fusion(bf16[128,3072]{0,1:T(8,128)(2,1)S(1)} %copy.84, s32[3072]{0:T(1024)S(1)} %broadcast_clamp_fusion.1), kind=kCustom, calls=%fused_computation.4 | custom fusion | bytes 1585152 | tf_op jit(solution)/shard_map/jit(_take)/gather | solution.py:105
  40.0 3.1 copy.80
  43.2 2.7 all-to-all-start.1
  45.9 5.1 copy.105
  51.0 3.1 copy.106
  54.2 4.3 gather_fusion.1
  58.5 4.5 copy.81
  63.0 4.4 gather_fusion.2
  67.4 4.6 copy.82
  72.2 34.0 %all-to-all-done.1 = bf16[32,4,24,256]{3,2,1,0:T(8,128)(2,1)S(1)} async-done(((bf16[32,4,24,256]{3,2,1,0:T(8,128)(2,1)}), bf16[32,4,24,256]{3,2,1,0:T(8,128)(2,1)S(1)}, u32[]{:S(2)}, u32[]{:S(2)}) %all-to-all-start.1) | async-done | bytes 1572896 | tf_op jit(solution)/shard_map/all_to_all | solution.py:109
  107.4 2.1 gather_fusion.3
  109.7 50.7 %all-gather.12.cloned.1.call-done = bf16[1024,3072]{0,1:T(8,128)(2,1)} async-done(((bf16[128,3072]{0,1:T(8,128)(2,1)}), bf16[1024,3072]{0,1:T(8,128)(2,1)}) %all-gather.12.cloned.1.call-update) | async-done | bytes 6291472 | tf_op jit(solution)/shard_map/all_gather | solution.py:106
  161.9 3.5 all-to-all-start.2
  167.9 56.2 %all-gather.6.cloned.1.call-done = bf16[3,3072,256]{1,2,0:T(8,128)(2,1)} async-done(((bf16[3,768,256]{1,2,0:T(8,128)(2,1)}), bf16[3,3072,256]{1,2,0:T(8,128)(2,1)}) %all-gather.6.cloned.1.call-update) | async-done | bytes 4718608 | tf_op jit(solution)/shard_map/all_gather | solution.py:125
  224.1 8.5 %fusion.12 = bf16[3,1024,256]{1,2,0:T(8,128)(2,1)S(1)} fusion(bf16[3,3072,256]{1,2,0:T(8,128)(2,1)} %all-gather.6.cloned.1.call-done, bf16[1024,3072]{0,1:T(8,128)(2,1)} %all-gather.12.cloned.1.call-done), kind=kOutput, calls=%fused_computation.28 | convolution fusion | flops 4832624640 | bytes 12582912 | tf_op jit(solution)/shard_map/sr,mrc->msc/dot_general | solution.py:126
  233.9 8.7 %fusion.22 = (f32[2,1024]{1,0:T(2,128)S(1)}, f32[2,1024,1024]{1,2,0:T(8,128)}) fusion(pred[1024,1024]{0,1:T(8,128)(4,1)S(1)} %fusion.6, bf16[1024,2,128]{0,2,1:T(8,128)(2,1)} %bitcast.102, bf16[1024,2,128]{0,2,1:T(8,128)(2,1)} %bitcast.101), kind=kOutput, calls=%fused_computation.60 | convolution fusion | flops 547357696 | bytes 10493952 | tf_op jit(solution)/shard_map/sub | solution.py:140
  242.5 4.3 fusion.15
  246.9 3.8 all-gather.8.cloned.1.call-done
  250.7 5.9 %convolution_convert_fusion = bf16[1024,3072]{1,0:T(8,128)(2,1)} fusion(bf16[1024,256]{0,1:T(8,128)(2,1)S(1)} %bitcast.99, bf16[3072,256]{1,0:T(8,128)(2,1)} %all-gather.8.cloned.1.call-done), kind=kOutput, calls=%fused_computation.15 | convolution fusion | flops 1613758464 | bytes 8388608 | tf_op jit(solution)/shard_map/sc,rc->sr/dot_general | solution.py:144
  257.1 119.5 %reduce-scatter.2.cloned.1.call-done = bf16[128,3072]{1,0:T(8,128)(2,1)} async-done(((bf16[1024,3072]{1,0:T(8,128)(2,1)}), bf16[128,3072]{1,0:T(8,128)(2,1)}) %reduce-scatter.2.cloned.1.call-update) | async-done | bytes 786448 | tf_op jit(solution)/shard_map/reduce_scatter | solution.py:158
  378.0 11.5 %gather_fusion.7 = bf16[3072,128]{1,0:T(8,128)(2,1)} fusion(bf16[128,3072]{0,1:T(8,128)(2,1)S(1)} %copy.94, s32[3072]{0:T(1024)S(1)} %broadcast_clamp_fusion), kind=kCustom, calls=%fused_computation.7 | custom fusion | bytes 1585152 | tf_op jit(solution)/shard_map/jit(_take)/gather | solution.py:161
  391.2 2.5 multiply_convert_fusion
  393.7 4.2 all-to-all-start.3
  397.9 149.0 %all-gather.10.cloned.1.call-done = bf16[1024,3072]{0,1:T(8,128)(2,1)} async-done(((bf16[128,3072]{0,1:T(8,128)(2,1)}), bf16[1024,3072]{0,1:T(8,128)(2,1)}) %all-gather.10.cloned.1.call-update) | async-done | bytes 6291472 | tf_op jit(solution)/shard_map/all_gather | solution.py:167
  546.9 10.7 %fusion.23 = (f32[1024]{0:T(1024)S(1)}, f32[1024,1024]{0,1:T(8,128)S(1)}) fusion(bf16[1024,3072]{0,1:T(8,128)(2,1)} %all-gather.10.cloned.1.call-done, bf16[3072,1024]{1,0:T(8,128)(2,1)} %param.19), kind=kOutput, calls=%fused_computation.61 | convolution fusion | flops 6443498496 | bytes 16781312 | tf_op jit(solution)/shard_map/dot_general | solution.py:168
  559.7 4.7 all-to-all-start.4
  565.6 4.3 gather_fusion.5
  569.9 3.9 copy.91
  573.8 4.3 gather_fusion.6
  578.1 3.9 copy.92
  (62 shorter events, 21.2 us)
Async XLA Ops:
  9.9 14.6 %all-to-all-start = ((s32[32,1,258]{2,1,0:T(1,128)}), s32[32,1,258]{2,1,0:T(1,128)S(1)}, u32[]{:S(2)}, u32[]{:S(2)}) async-start(s32[32,1,258]{2,1,0:T(1,128)} %broadcast_in_dim.85), calls=%async_computation | async-start | bytes 98304 | tf_op jit(solution)/shard_map/all_to_all | solution.py:47
  17.2 143.2 %all-gather.12.cloned.1.call-start = ((), (), s32[]{:S(2)}) async-start(), calls=%async_computation.10 | async-start | bytes 7077888 | tf_op jit(solution)/shard_map/all_gather | solution.py:106
  24.4 11.8 %copy-start.2 = (s32[32,1,258]{2,1,0:T(1,128)}, s32[32,1,258]{2,1,0:T(1,128)S(1)}, u32[]{:S(2)}) copy-start(s32[32,1,258]{2,1,0:T(1,128)S(1)} %all-to-all-done) | copy-start | bytes 99076
  43.2 63.1 %all-to-all-start.1 = ((bf16[32,4,24,256]{3,2,1,0:T(8,128)(2,1)}), bf16[32,4,24,256]{3,2,1,0:T(8,128)(2,1)S(1)}, u32[]{:S(2)}, u32[]{:S(2)}) async-start(bf16[32,4,24,256]{3,2,1,0:T(8,128)(2,1)} %bitcast.1), calls=%async_computation.1 | async-start | bytes 3145728 | tf_op jit(solution)/shard_map/all_to_all | solution.py:109
  45.9 178.3 %all-gather.6.cloned.1.call-start = ((), (), s32[]{:S(2)}) async-start(), calls=%async_computation.6 | async-start | bytes 5898240 | tf_op jit(solution)/shard_map/all_gather | solution.py:125
  45.9 5.1 copy-start.1
  106.3 1.1 copy-start
  161.9 94.7 %all-to-all-start.2 = ((f32[32,4,24,256]{3,2,1,0:T(8,128)}), f32[32,4,24,256]{3,2,1,0:T(8,128)}, u32[]{:S(2)}, u32[]{:S(2)}) async-start(f32[32,4,24,256]{3,2,1,0:T(8,128)} %bitcast.81), calls=%async_computation.2 | async-start | bytes 6291456 | tf_op jit(solution)/shard_map/all_to_all | solution.py:124
  165.5 85.2 %all-gather.8.cloned.1.call-start = ((), (), s32[]{:S(2)}) async-start(), calls=%async_computation.7 | async-start | bytes 1966080 | tf_op jit(solution)/shard_map/all_gather | solution.py:147
  167.7 208.8 %reduce-scatter.2.cloned.1.call-start = ((), (), s32[]{:S(2)}) async-start(), calls=%async_computation.8 | async-start | bytes 7077888 | tf_op jit(solution)/shard_map/reduce_scatter | solution.py:158
  256.6 290.3 %all-gather.10.cloned.1.call-start = ((), (), s32[]{:S(2)}) async-start(), calls=%async_computation.9 | async-start | bytes 7077888 | tf_op jit(solution)/shard_map/all_gather | solution.py:167
  378.0 13.1 %copy-start.3 = (f32[3072]{0:T(1024)S(1)}, f32[3072]{0:T(1024)}, u32[]{:S(2)}) copy-start(f32[3072]{0:T(1024)} %param.18) | copy-start | bytes 36868
  393.7 166.0 %all-to-all-start.3 = ((f32[32,4,24,256]{3,2,1,0:T(8,128)}), f32[32,4,24,256]{3,2,1,0:T(8,128)}, u32[]{:S(2)}, u32[]{:S(2)}) async-start(f32[32,4,24,256]{3,2,1,0:T(8,128)} %bitcast.80), calls=%async_computation.3 | async-start | bytes 6291456 | tf_op jit(solution)/shard_map/all_to_all | solution.py:157
  559.7 22.3 %all-to-all-start.4 = ((f32[8,3,128]{2,1,0:T(4,128)}), f32[8,3,128]{2,1,0:T(4,128)S(1)}, u32[]{:S(2)}, u32[]{:S(2)}) async-start(f32[8,3,128]{2,1,0:T(4,128)} %maximum_bitcast_fusion), calls=%async_computation.5 | async-start | bytes 32768 | tf_op jit(solution)/shard_map/all_to_all | solution.py:63
Sparse Core Ops, SparseCore 0:
  36.3 124.0 all-gather.11
  162.5 61.5 all-gather.5
  225.7 24.9 all-gather.7
  256.7 119.7 reduce-scatter.1
  393.8 153.0 all-gather.9
